TPU v7x, 512 devices: a whole 4x8x8 slice. The times are simulated.
512 devices in a mesh: gz: 8 (over z_lo, core), pa: 64 (over y, z_hi, x).
Axes of the slice: x: 4, y: 8, z: 8 (z_hi: 2, z_lo: 4; z = z_hi * 4 + z_lo), core: 2. Of those that a mesh axis runs over, the one named last changes fastest.
Arguments:
- velocity: float32 [3, 8, 2, 512, 1024], P(None, 'gz', None, 'pa'), may hold values from -3 to 3
- mode_mask: int32 [512, 1024], P('pa'), may hold values from 0 to 1, as said below
Outputs:
- velocity_next: float32 [3, 8, 2, 512, 1024], P(None, 'gz', None, 'pa')
- divergence: float32 [8, 2, 512, 1024], P('gz', None, 'pa')
Inputs may be any that keep to these rules, and one draw needn't show every extreme that they name: mode_mask is 1 exactly where |s(m)| <= A and n <= B, for one A from 256 to 340 and one B from 256 to 340 in each draw, and 0 elsewhere.
All inputs are finite; a program needn't handle non-finite values.
Results may differ from a plain program's by a relative error of at most 0.00005.
Values sent between devices are 32-bit elements; how exact they have to be, the bound alone decides.
A program may use at most 64 MiB of HBM per device.

v0:
```python
import math

import jax
import jax.numpy as jnp
import numpy as np
from jax import lax
from jax.experimental import pallas as pl
from jax.experimental.pallas import tpu as pltpu
from jax.sharding import PartitionSpec as P


TWO_PI = 2.0 * math.pi
TIME_STEP = 0.2
VISCOSITY = 0.25
RANKS = 64
LAST_RANK = 42
F32 = jnp.float32
BF16 = jnp.bfloat16


def halves(table):
    table = np.asarray(table, np.float32)
    high = table.astype(jnp.bfloat16)
    low = (table - high.astype(np.float32)).astype(jnp.bfloat16)
    return np.stack([high, low])


def tables():
    index = np.arange
    p, b, c, s, q, r = index(64), index(128), index(8), index(8), index(64), index(128)
    d = (2 * p[None, :] + index(2)[:, None]).reshape(-1)
    angle = TWO_PI / 128.0 * (d[:, None] * b[None, :] % 128)
    cos, sin = np.cos(angle) / 32.0, np.sin(angle) / 32.0
    x_in = np.block([[cos, -sin], [sin, cos]])
    angle = TWO_PI / 1024.0 * (c[:, None] * b[None, :])
    x_turn = np.stack([np.cos(angle), np.sin(angle)]).astype(np.float32).reshape(2, 8, 1, 128)
    angle = TWO_PI / 128.0 * (r[:, None] * q[None, :] % 128)
    cos, sin = np.cos(angle) / 32.0, np.sin(angle) / 32.0
    y_in = np.block([[cos, -sin], [sin, cos]])
    angle = TWO_PI / 1024.0 * (r[:, None] * np.tile(s, 16)[None, :])
    y_turn = np.stack([np.cos(angle), np.sin(angle)]).astype(np.float32)
    angle = TWO_PI / 8.0 * (s[:, None] * s[None, :] % 8)
    cos8, sin8 = np.cos(angle), np.sin(angle)
    eye = np.eye(8)
    real = np.kron(np.eye(2), np.kron(eye, cos8))
    imag = np.kron(np.eye(2), np.kron(eye, -sin8))
    both = np.concatenate([real, imag], 0)
    y_grid = np.concatenate([both, np.roll(both, 64, axis=1)], 1)
    real = np.kron(eye, cos8) / 32.0
    imag = np.kron(eye, -sin8) / 32.0
    line = np.concatenate([real, imag, imag, -real], 1)
    y_low = np.concatenate([line, np.zeros_like(line)], 0)
    y_diff = np.concatenate([line, -line], 0)
    angle = TWO_PI / 128.0 * (q[:, None] * r[None, :] % 128)
    y_out = np.concatenate([np.cos(angle), np.sin(angle)], 1)
    angle = TWO_PI / 128.0 * (d[:, None] * b[None, :] % 128)
    x_out = np.concatenate([np.cos(angle), np.sin(angle)], 1) / 32.0
    return dict(
        x_in=halves(x_in),
        x_turn=x_turn,
        y_in=halves(y_in),
        y_turn=y_turn,
        y_grid=halves(y_grid),
        y_low=halves(y_low),
        y_diff=halves(y_diff),
        y_out=halves(y_out),
        x_out=halves(x_out),
    )


NAMES = ("x_in", "x_turn", "y_in", "y_turn", "y_grid", "y_low", "y_diff", "y_out", "x_out")


def split(value):
    high = value.astype(BF16)
    return high, (value - high.astype(F32)).astype(BF16)


def dot(left, right, contract=((1,), (0,))):
    def one(i, j):
        return lax.dot_general(left[i], right[j], (contract, ((), ())), preferred_element_type=F32)

    return one(0, 0) + (one(0, 1) + one(1, 0))


def eight(values, sign):
    count = len(values)
    if count == 1:
        return values
    even, odd = eight(values[0::2], sign), eight(values[1::2], sign)
    half = count // 2
    low, high = [], []
    for k in range(half):
        (er, ei), (qr, qi) = even[k], odd[k]
        turn = 8 // count * k
        if turn == 0:
            tr, ti = qr, qi
        elif turn == 2:
            tr, ti = -sign * qi, sign * qr
        else:
            root = math.sqrt(0.5)
            if turn == 1:
                tr, ti = root * (qr - sign * qi), root * (qi + sign * qr)
            else:
                tr, ti = -root * (qr + sign * qi), root * (sign * qr - qi)
        low.append((er + tr, ei + ti))
        high.append((er - tr, ei - ti))
    return low + high


def x_inverse(fields, turn_cos, turn_sin, table):
    real, imag = [], []
    for field in fields:
        for c, (vr, vi) in enumerate(eight(field, 1.0)):
            real.append(vr * turn_cos[c] - vi * turn_sin[c])
            imag.append(vr * turn_sin[c] + vi * turn_cos[c])
    lines = jnp.concatenate([jnp.concatenate(real, 0), jnp.concatenate(imag, 0)], 1)
    return dot(table, split(lines), ((1,), (1,)))


def y_turned(modes, cos, sin, table):
    lines = dot(table, split(modes))
    out = []
    for k in range(modes.shape[1] // 128):
        vr, vi = lines[:128, 128 * k : 128 * k + 128], lines[128:, 128 * k : 128 * k + 128]
        out.append(jnp.concatenate([vr * cos - vi * sin, vr * sin + vi * cos], 1))
    return out


def y_forward(product, cos, sin, table):
    line = dot(split(product), table)
    one, two = line[:, :128], line[:, 128:]
    return jnp.concatenate([one * cos + two * sin, two * cos - one * sin], 0)


def x_forward(block, turn_cos, turn_sin, table):
    line = dot(split(block.T), table)
    values = []
    for c in range(8):
        re, im = line[8 * c : 8 * c + 8], line[64 + 8 * c : 72 + 8 * c]
        vr, vi = re[:, :128] + im[:, 128:], im[:, :128] - re[:, 128:]
        values.append((vr * turn_cos[c] + vi * turn_sin[c], vi * turn_cos[c] - vr * turn_sin[c]))
    return eight(values, -1.0)


def step(index):
    return (1 - 2 * lax.rem(index, 2)) * lax.div(index + 1, 2)


def partner(me, index):
    dz = 1 - lax.rem(index, 2)
    dx = 2 + step(lax.rem(lax.div(index, 2), 4))
    dy = 4 + step(lax.div(index, 8))
    x = lax.rem(lax.rem(me, 4) + dx, 4)
    z = lax.rem(lax.rem(lax.div(me, 4), 2) + dz, 2)
    y = lax.rem(lax.div(me, 8) + dy, 8)
    return (y * 2 + z) * 4 + x


def rows(start, count):
    return pl.ds(pl.multiple_of(start, count if count != 6 else 8), count)


def kernel(vel, mask, x_in, x_turn, y_in, y_turn, y_grid, y_low, y_diff, y_out, x_out, out, div,
           send_a, recv_a, send_b, recv_b, send_c, recv_c, low, high, w_low, w_high, w_send,
           a_sems, b_sems, c_sems, low_send, low_recv, high_send, high_recv, w_sems):
    me, plane = lax.axis_index("pa"), lax.axis_index("gz")
    barrier = pltpu.get_barrier_semaphore()

    def hello(i, _):
        pl.semaphore_signal(barrier, inc=1, device_id={"gz": plane, "pa": partner(me, i)})
        return 0

    lax.fori_loop(0, RANKS - 1, hello, 0)
    has_low, has_high = plane > 0, plane < 7

    @pl.when(has_low)
    def _():
        pl.semaphore_signal(barrier, inc=1, device_id={"gz": plane - 1, "pa": me})

    @pl.when(has_high)
    def _():
        pl.semaphore_signal(barrier, inc=1, device_id={"gz": plane + 1, "pa": me})

    sub = lax.broadcasted_iota(jnp.int32, (8, 128), 0)
    lane = lax.broadcasted_iota(jnp.int32, (8, 128), 1)
    modes = me * 8 + sub
    ky = (TWO_PI / 1024.0) * modes.astype(F32)
    weight = jnp.where(modes == 0, 1.0, 2.0).astype(F32)

    def kx(a):
        return (TWO_PI / 1024.0) * (lane + (128 * a - 1024 * (a // 4))).astype(F32)

    def piece(ref, *lead):
        return [ref[(*lead, slice(None), pl.ds(128 * a, 128))] for a in range(8)]

    turn_cos = [weight * x_turn[0, c] for c in range(8)]
    turn_sin = [weight * x_turn[1, c] for c in range(8)]

    def field(comp):
        return list(zip(piece(vel, comp, 0, 0), piece(vel, comp, 0, 1), strict=True))

    u, v, w = field(0), field(1), field(2)
    omega_z = [
        (ky * u[a][1] - kx(a) * v[a][1], kx(a) * v[a][0] - ky * u[a][0]) for a in range(8)
    ]
    grid = x_inverse([u, v, w, omega_z], turn_cos, turn_sin, x_in)
    for k in range(2):
        for j in range(4):
            send_a[pl.ds(4 * k + j, 64, stride=8), :] = grid[64 * j : 64 * j + 64, 128 * k : 128 * k + 128]

    @pl.when(jnp.logical_and(has_low, has_high))
    def _():
        pl.semaphore_wait(barrier, RANKS + 1)

    @pl.when(jnp.logical_not(jnp.logical_and(has_low, has_high)))
    def _():
        pl.semaphore_wait(barrier, RANKS)

    def to_low(group):
        comps = pl.ds(0, 2) if group == 0 else pl.ds(2, 1)
        return pltpu.make_async_remote_copy(
            vel.at[comps, 0], high.at[comps], low_send.at[group], high_recv.at[group],
            device_id={"gz": plane - 1, "pa": me})

    def to_high(group):
        comps = pl.ds(0, 2) if group == 0 else pl.ds(2, 1)
        return pltpu.make_async_remote_copy(
            vel.at[comps, 0], low.at[comps], high_send.at[group], low_recv.at[group],
            device_id={"gz": plane + 1, "pa": me})

    @pl.when(has_low)
    def _():
        to_low(0).start()

    @pl.when(has_high)
    def _():
        to_high(0).start()

    def send(source, target, sems, count, stride, dest):
        return pltpu.make_async_remote_copy(
            source.at[rows(dest * stride, count)], target.at[rows(me * stride, count)],
            sems.at[0], sems.at[1], device_id={"gz": plane, "pa": dest})

    def start_a(i, _):
        send(send_a, recv_a, a_sems, 8, 8, partner(me, i)).start()
        return 0

    lax.fori_loop(0, RANKS - 1, start_a, 0)

    @pl.when(has_low)
    def _():
        to_low(1).start()
        pltpu.make_async_copy(low.at[pl.ds(0, 2)], low.at[pl.ds(0, 2)], low_recv.at[0]).wait()

    @pl.when(jnp.logical_not(has_low))
    def _():
        low[...] = jnp.zeros_like(low)
        w_low[...] = jnp.zeros_like(w_low)

    @pl.when(has_high)
    def _():
        to_high(1).start()
        pltpu.make_async_copy(high.at[pl.ds(0, 2)], high.at[pl.ds(0, 2)], high_recv.at[0]).wait()

    @pl.when(jnp.logical_not(has_high))
    def _():
        high[...] = jnp.zeros_like(high)
        w_high[...] = jnp.zeros_like(w_high)

    def slope(comp):
        pairs = []
        for a in range(8):
            at = pl.ds(128 * a, 128)
            pairs.append(tuple(0.5 * (high[comp, i, :, at] - low[comp, i, :, at]) for i in range(2)))
        return pairs

    dz_u, dz_v = slope(0), slope(1)
    w = field(2)
    omega_x = [(-(ky * w[a][1]) - dz_v[a][0], ky * w[a][0] - dz_v[a][1]) for a in range(8)]
    omega_y = [(dz_u[a][0] + kx(a) * w[a][1], dz_u[a][1] - kx(a) * w[a][0]) for a in range(8)]
    grid = x_inverse([omega_x, omega_y], turn_cos, turn_sin, x_in)
    for j in range(4):
        send_b[pl.ds(j, 64, stride=4), :] = grid[64 * j : 64 * j + 64]

    def start_b(i, _):
        send(send_b, recv_b, b_sems, 4, 4, partner(me, i)).start()
        return 0

    lax.fori_loop(0, RANKS - 1, start_b, 0)
    recv_a[rows(me * 8, 8), :] = send_a[rows(me * 8, 8), :]
    recv_b[rows(me * 4, 4), :] = send_b[rows(me * 4, 4), :]

    def wait_all(ref, sem, count):
        view = ref.at[pl.ds(0, count)]
        pltpu.make_async_copy(view, view, sem).wait()

    cos, sin = y_turn[0], y_turn[1]
    wait_all(recv_a, a_sems.at[1], 8 * (RANKS - 1))

    def gathered(ref, stride, base, e):
        return jnp.concatenate(
            [ref[pl.ds(base + e, 64, stride=stride), :], ref[pl.ds(base + 2 + e, 64, stride=stride), :]], 0)

    first = y_turned(
        jnp.concatenate([gathered(recv_a, 8, 4 * k, e) for k in range(2) for e in range(2)], 1), cos, sin, y_in)
    first = [dot(split(value), y_grid) for value in first]
    wait_all(recv_b, b_sems.at[1], 4 * (RANKS - 1))
    second = y_turned(jnp.concatenate([gathered(recv_b, 4, 0, e) for e in range(2)], 1), cos, sin, y_in)
    second = [dot(split(value), y_grid) for value in second]

    def last(parts):
        return dot(y_out, split(jnp.concatenate(parts, 1)))

    products = [[], [], []]
    for e in range(2):
        uv, wz, xy = first[e], first[2 + e], second[e]
        uv, vu = uv[:, :128], uv[:, 128:]
        wz, zw = wz[:, :128], wz[:, 128:]
        xy, yx = xy[:, :128], xy[:, 128:]
        products[0].append(vu * zw - wz * yx)
        products[1].append(wz * xy - uv * zw)
        products[2].append(uv * yx)
    for comp in range(3):
        table = y_diff if comp == 2 else y_low
        spectral = last([y_forward(value, cos, sin, table) for value in products[comp]])
        for e in range(2):
            send_c[pl.ds(2 * comp + e, 64, stride=8), :] = spectral[:, 128 * e : 128 * e + 128]

    def start_c(i, _):
        dest = partner(me, i)

        @pl.when(dest <= LAST_RANK)
        def _():
            send(send_c, recv_c, c_sems, 6, 8, dest).start()

        return 0

    lax.fori_loop(0, RANKS - 1, start_c, 0)
    inside = me <= LAST_RANK

    @pl.when(has_low)
    def _():
        pltpu.make_async_copy(low.at[pl.ds(2, 1)], low.at[pl.ds(2, 1)], low_recv.at[1]).wait()

    @pl.when(has_high)
    def _():
        pltpu.make_async_copy(high.at[pl.ds(2, 1)], high.at[pl.ds(2, 1)], high_recv.at[1]).wait()

    for comp in range(3):
        for i in range(2):
            for a in range(8):
                at = pl.ds(128 * a, 128)
                mid = vel[comp, 0, i, :, at]
                viscous = (high[comp, i, :, at] - 2.0 * mid + low[comp, i, :, at]) - (kx(a) * kx(a) + ky * ky) * mid
                out[comp, 0, i, :, at] = mid + (TIME_STEP * VISCOSITY) * viscous

    @pl.when(inside)
    def _():
        recv_c[rows(me * 8, 6), :] = send_c[rows(me * 8, 6), :]
        wait_all(recv_c, c_sems.at[1], 6 * (RANKS - 1))
        plain_cos = [jnp.broadcast_to(x_turn[0, c], (8, 128)) for c in range(8)]
        plain_sin = [jnp.broadcast_to(x_turn[1, c], (8, 128)) for c in range(8)]
        for comp in range(3):
            block = jnp.concatenate([recv_c[pl.ds(2 * comp + e, 64, stride=8), :] for e in range(2)], 0)
            for a, pair in enumerate(x_forward(block, plain_cos, plain_sin, x_out)):
                at = pl.ds(128 * a, 128)
                keep = mask[:, at].astype(F32) * TIME_STEP
                for i in range(2):
                    out[comp, 0, i, :, at] = out[comp, 0, i, :, at] + pair[i] * keep

    w_send[...] = out[2, 0]

    def w_to_low():
        return pltpu.make_async_remote_copy(
            w_send, w_high, w_sems.at[0], w_sems.at[1], device_id={"gz": plane - 1, "pa": me})

    def w_to_high():
        return pltpu.make_async_remote_copy(
            w_send, w_low, w_sems.at[2], w_sems.at[3], device_id={"gz": plane + 1, "pa": me})

    @pl.when(has_low)
    def _():
        w_to_low().start()

    @pl.when(has_high)
    def _():
        w_to_high().start()

    for a in range(8):
        at = pl.ds(128 * a, 128)
        div[0, 0, :, at] = -(kx(a) * out[0, 0, 1, :, at]) - ky * out[1, 0, 1, :, at]
        div[0, 1, :, at] = kx(a) * out[0, 0, 0, :, at] + ky * out[1, 0, 0, :, at]

    @pl.when(has_low)
    def _():
        pltpu.make_async_copy(w_low, w_low, w_sems.at[3]).wait()

    @pl.when(has_high)
    def _():
        pltpu.make_async_copy(w_high, w_high, w_sems.at[1]).wait()

    div[0] = div[0] + 0.5 * (w_high[...] - w_low[...])

    wait_all(send_a, a_sems.at[0], 8 * (RANKS - 1))
    wait_all(send_b, b_sems.at[0], 4 * (RANKS - 1))

    @pl.when(inside)
    def _():
        wait_all(send_c, c_sems.at[0], 6 * LAST_RANK)

    @pl.when(jnp.logical_not(inside))
    def _():
        wait_all(send_c, c_sems.at[0], 6 * (LAST_RANK + 1))

    @pl.when(has_low)
    def _():
        to_low(0).wait_send()
        to_low(1).wait_send()
        w_to_low().wait_send()

    @pl.when(has_high)
    def _():
        to_high(0).wait_send()
        to_high(1).wait_send()
        w_to_high().wait_send()


def on_device(velocity, mode_mask):
    constants = tables()
    whole = pl.BlockSpec(memory_space=pltpu.VMEM)
    dma, vmem = pltpu.SemaphoreType.DMA, pltpu.VMEM
    return pl.pallas_call(
        kernel,
        name="substep",
        out_shape=(
            jax.ShapeDtypeStruct((3, 1, 2, 8, 1024), F32),
            jax.ShapeDtypeStruct((1, 2, 8, 1024), F32),
        ),
        in_specs=[whole] * (2 + len(NAMES)),
        out_specs=(whole, whole),
        scratch_shapes=[
            vmem((512, 128), F32), vmem((512, 128), F32),
            vmem((256, 128), F32), vmem((256, 128), F32),
            vmem((512, 128), F32), vmem((512, 128), F32),
            vmem((3, 2, 8, 1024), F32), vmem((3, 2, 8, 1024), F32),
            vmem((2, 8, 1024), F32), vmem((2, 8, 1024), F32), vmem((2, 8, 1024), F32),
            dma((2,)), dma((2,)), dma((2,)),
            dma((2,)), dma((2,)), dma((2,)), dma((2,)), dma((4,)),
        ],
        compiler_params=pltpu.CompilerParams(collective_id=0, has_side_effects=True),
    )(velocity, mode_mask, *(jnp.asarray(constants[name]) for name in NAMES))


def solution(mesh):
    return jax.shard_map(
        on_device,
        mesh=mesh,
        in_specs=(P(None, "gz", None, "pa", None), P("pa", None)),
        out_specs=(P(None, "gz", None, "pa", None), P("gz", None, "pa", None)),
        check_vma=False,
    )
```

profile of v0, /device:TPU:65, one launch (start us, length us, event | category | flops | bytes accessed | tf_op | source)
XLA Modules:
  0.0 56.8 jit_solution(6335245535028370372)
XLA Ops:
  0.6 53.9 %substep.1 = (f32[3,1,2,8,1024]{4,3,2,1,0:T(8,128)}, f32[1,2,8,1024]{3,2,1,0:T(8,128)}) custom-call(f32[3,1,2,8,1024]{4,3,2,1,0:T(8,128)} %vel.1, s32[8,1024]{1,0:T(8,128)} %mask.1, bf16[2,256,256]{2,1,0:T(8,128)(2,1)} %constant.18.clone.x_in, f32[2,8,1,128]{3,2,1,0:T(1,128)} %constant.19.clone.x_turn, bf16[2,256,128]{2,1,0:T(8,128)(2,1)} %constant.20.clone.y_in, ...), custom_call_target="tpu_custom_call" | custom-call | tf_op jit(solution)/shard_map/substep/pallas_call | solution.py:433
  54.5 0.0 copy-start
  54.5 1.6 %copy.15 = f32[3,1,2,8,1024]{4,3,2,1,0:T(8,128)} copy(f32[3,1,2,8,1024]{4,3,2,1,0:T(8,128)} %get-tuple-element.4) | data formatting | bytes 393216
  56.2 0.0 copy-done
  56.2 0.6 %copy.16 = f32[1,2,8,1024]{3,2,1,0:T(8,128)} copy(f32[1,2,8,1024]{3,2,1,0:T(8,128)S(1)} %copy-done) | data formatting | bytes 131072
Async XLA Ops:
  54.5 1.7 %copy-start = (f32[1,2,8,1024]{3,2,1,0:T(8,128)S(1)}, f32[1,2,8,1024]{3,2,1,0:T(8,128)}, u32[]{:S(2)}) copy-start(f32[1,2,8,1024]{3,2,1,0:T(8,128)} %get-tuple-element.5) | copy-start | bytes 196612
where the time goes:
time: 57 us; the launch traced here: 56.8 us
  Pallas kernels  53.9 us (95%)
  local copies, waits for them, and re-layouts  2.28 us (4%)
  between operations  0.65 us (1%)
    pallas_call x1, Pallas kernels, on_device(): pl.pallas_call(kernel, name='substep', out_shape=(jax.ShapeDtypeStruct((3...  53.9 us
    unnamed x4, local copies, waits for them, and re-layouts  2.28 us

commit v1 on v0

--- a/solution.py
+++ b/solution.py
@@ -161,11 +161,24 @@
     return pl.ds(pl.multiple_of(start, count if count != 6 else 8), count)
 
 
-def kernel(vel, mask, x_in, x_turn, y_in, y_turn, y_grid, y_low, y_diff, y_out, x_out, out, div,
+def kernel(*refs):
+    count = 2 + len(NAMES)
+    sources, out, div, held = refs[:count], refs[count], refs[count + 1], refs[count + 2 : 2 * count + 2]
+    body(sources, held, out, div, *refs[2 * count + 2 :])
+
+
+def body(sources, held, out, div, load_sems,
            send_a, recv_a, send_b, recv_b, send_c, recv_c, low, high, w_low, w_high, w_send,
            a_sems, b_sems, c_sems, low_send, low_recv, high_send, high_recv, w_sems):
     me, plane = lax.axis_index("pa"), lax.axis_index("gz")
     barrier = pltpu.get_barrier_semaphore()
+    vel, mask, x_in, x_turn, y_in, y_turn, y_grid, y_low, y_diff, y_out, x_out = held
+
+    def load(i):
+        return pltpu.make_async_copy(sources[i], held[i], load_sems.at[i])
+
+    for i in (0, 2, 3):
+        load(i).start()
 
     def hello(i, _):
         pl.semaphore_signal(barrier, inc=1, device_id={"gz": plane, "pa": partner(me, i)})
@@ -182,6 +195,9 @@
     def _():
         pl.semaphore_signal(barrier, inc=1, device_id={"gz": plane + 1, "pa": me})
 
+    rest = [i for i in range(len(held)) if i not in (0, 2, 3)]
+    for i in rest:
+        load(i).start()
     sub = lax.broadcasted_iota(jnp.int32, (8, 128), 0)
     lane = lax.broadcasted_iota(jnp.int32, (8, 128), 1)
     modes = me * 8 + sub
@@ -194,6 +210,8 @@
     def piece(ref, *lead):
         return [ref[(*lead, slice(None), pl.ds(128 * a, 128))] for a in range(8)]
 
+    for i in (0, 2, 3):
+        load(i).wait()
     turn_cos = [weight * x_turn[0, c] for c in range(8)]
     turn_sin = [weight * x_turn[1, c] for c in range(8)]
 
@@ -295,6 +313,8 @@
         view = ref.at[pl.ds(0, count)]
         pltpu.make_async_copy(view, view, sem).wait()
 
+    for i in rest:
+        load(i).wait()
     cos, sin = y_turn[0], y_turn[1]
     wait_all(recv_a, a_sems.at[1], 8 * (RANKS - 1))
 
@@ -428,18 +448,20 @@
 
 def on_device(velocity, mode_mask):
     constants = tables()
+    operands = (velocity, mode_mask, *(jnp.asarray(constants[name]) for name in NAMES))
     whole = pl.BlockSpec(memory_space=pltpu.VMEM)
     dma, vmem = pltpu.SemaphoreType.DMA, pltpu.VMEM
     return pl.pallas_call(
         kernel,
         name="substep",
         out_shape=(
-            jax.ShapeDtypeStruct((3, 1, 2, 8, 1024), F32),
-            jax.ShapeDtypeStruct((1, 2, 8, 1024), F32),
+            vmem((3, 1, 2, 8, 1024), F32),
+            vmem((1, 2, 8, 1024), F32),
         ),
-        in_specs=[whole] * (2 + len(NAMES)),
+        in_specs=[pl.BlockSpec(memory_space=pl.ANY)] * len(operands),
         out_specs=(whole, whole),
         scratch_shapes=[
+            *(vmem(operand.shape, operand.dtype) for operand in operands), dma((len(operands),)),
             vmem((512, 128), F32), vmem((512, 128), F32),
             vmem((256, 128), F32), vmem((256, 128), F32),
             vmem((512, 128), F32), vmem((512, 128), F32),
@@ -449,7 +471,7 @@
             dma((2,)), dma((2,)), dma((2,)), dma((2,)), dma((4,)),
         ],
         compiler_params=pltpu.CompilerParams(collective_id=0, has_side_effects=True),
-    )(velocity, mode_mask, *(jnp.asarray(constants[name]) for name in NAMES))
+    )(*operands)
 
 
 def solution(mesh):

time: 57 us -> 53.9 us (0.946)
  Pallas kernels: 53.9 us -> 51.8 us
  local copies, waits for them, and re-layouts: 2.28 us -> 1.31 us
    pallas_call x1, Pallas kernels: 53.9 us -> 51.8 us  [on_device(): pl.pallas_call(kernel, name='substep', out_shape=(vmem((3, 1, 2, 8, 1024)...]
    unnamed x4 -> x2, local copies, waits for them, and re-layouts: 2.28 us -> 1.31 us
where the time goes in v1:
time: 53.9 us; the launch traced here: 53.7 us
  Pallas kernels  51.8 us (96%)
  local copies, waits for them, and re-layouts  1.31 us (2%)
  between operations  0.64 us (1%)
    pallas_call x1, Pallas kernels, on_device(): pl.pallas_call(kernel, name='substep', out_shape=(vmem((3, 1, 2, 8, 1024)...  51.8 us
    unnamed x2, local copies, waits for them, and re-layouts  1.31 us

profile of v1, /device:TPU:65, one launch (start us, length us, event | category | flops | bytes accessed | tf_op | source)
XLA Modules:
  0.0 53.7 jit_solution(40461298813615520)
XLA Ops:
  0.6 51.8 %substep.1 = (f32[3,1,2,8,1024]{4,3,2,1,0:T(8,128)S(1)}, f32[1,2,8,1024]{3,2,1,0:T(8,128)S(1)}) custom-call(f32[3,1,2,8,1024]{4,3,2,1,0:T(8,128)} %refs_0_.1, s32[8,1024]{1,0:T(8,128)} %refs_1_.1, bf16[2,256,256]{2,1,0:T(8,128)(2,1)} %constant.18.clone.refs_2_, f32[2,8,1,128]{3,2,1,0:T(1,128)} %constant.19.clone.refs_3_, ...), custom_call_target="tpu_custom_call" | custom-call | tf_op jit(solution)/shard_map/substep/pallas_call | solution.py:454
  52.4 0.7 %copy.15 = f32[3,1,2,8,1024]{4,3,2,1,0:T(8,128)} copy(f32[3,1,2,8,1024]{4,3,2,1,0:T(8,128)S(1)} %get-tuple-element.2) | data formatting | bytes 393216
  53.1 0.6 %copy.16 = f32[1,2,8,1024]{3,2,1,0:T(8,128)} copy(f32[1,2,8,1024]{3,2,1,0:T(8,128)S(1)} %get-tuple-element.3) | data formatting | bytes 131072

commit v2 on v1

--- a/solution.py
+++ b/solution.py
@@ -13,6 +13,7 @@
 TIME_STEP = 0.2
 VISCOSITY = 0.25
 RANKS = 64
+WORKERS = 32
 LAST_RANK = 42
 F32 = jnp.float32
 BF16 = jnp.bfloat16
@@ -27,8 +28,8 @@
 
 def tables():
     index = np.arange
-    p, b, c, s, q, r = index(64), index(128), index(8), index(8), index(64), index(128)
-    d = (2 * p[None, :] + index(2)[:, None]).reshape(-1)
+    k, b, c, s, q, r = index(32), index(128), index(8), index(8), index(64), index(128)
+    d = (4 * k[None, :] + index(4)[:, None]).reshape(-1)
     angle = TWO_PI / 128.0 * (d[:, None] * b[None, :] % 128)
     cos, sin = np.cos(angle) / 32.0, np.sin(angle) / 32.0
     x_in = np.block([[cos, -sin], [sin, cos]])
@@ -148,17 +149,17 @@
 
 
 def partner(me, index):
-    dz = 1 - lax.rem(index, 2)
-    dx = 2 + step(lax.rem(lax.div(index, 2), 4))
-    dy = 4 + step(lax.div(index, 8))
-    x = lax.rem(lax.rem(me, 4) + dx, 4)
-    z = lax.rem(lax.rem(lax.div(me, 4), 2) + dz, 2)
-    y = lax.rem(lax.div(me, 8) + dy, 8)
-    return (y * 2 + z) * 4 + x
-
-
-def rows(start, count):
-    return pl.ds(pl.multiple_of(start, count if count != 6 else 8), count)
+    dx = 2 + step(lax.rem(index, 4))
+    dy = 4 + step(lax.div(index, 4))
+    return lax.rem(lax.div(me, 8) + dy, 8) * 4 + lax.rem(lax.rem(me, 4) + dx, 4)
+
+
+def rank(place, half):
+    return lax.div(place, 4) * 8 + half * 4 + lax.rem(place, 4)
+
+
+def rows(start, align, count):
+    return pl.ds(pl.multiple_of(start * align, align), count)
 
 
 def kernel(*refs):
@@ -180,12 +181,24 @@
     for i in (0, 2, 3):
         load(i).start()
 
-    def hello(i, _):
-        pl.semaphore_signal(barrier, inc=1, device_id={"gz": plane, "pa": partner(me, i)})
-        return 0
-
-    lax.fori_loop(0, RANKS - 1, hello, 0)
+    half = lax.rem(lax.div(me, 4), 2)
+    worker, late = half == 0, half == 1
+    place = lax.div(me, 8) * 4 + lax.rem(me, 4)
     has_low, has_high = plane > 0, plane < 7
+
+    def greet(dest):
+        pl.semaphore_signal(barrier, inc=1, device_id={"gz": plane, "pa": dest})
+
+    @pl.when(worker)
+    def _():
+        def hello(i, _):
+            spot = partner(me, i)
+            greet(rank(spot, 1))
+            greet(rank(spot, 0))
+            return 0
+
+        lax.fori_loop(0, WORKERS - 1, hello, 0)
+        greet(rank(place, 1))
 
     @pl.when(has_low)
     def _():
@@ -224,16 +237,11 @@
     ]
     grid = x_inverse([u, v, w, omega_z], turn_cos, turn_sin, x_in)
     for k in range(2):
-        for j in range(4):
-            send_a[pl.ds(4 * k + j, 64, stride=8), :] = grid[64 * j : 64 * j + 64, 128 * k : 128 * k + 128]
-
-    @pl.when(jnp.logical_and(has_low, has_high))
-    def _():
-        pl.semaphore_wait(barrier, RANKS + 1)
-
-    @pl.when(jnp.logical_not(jnp.logical_and(has_low, has_high)))
-    def _():
-        pl.semaphore_wait(barrier, RANKS)
+        for j in range(8):
+            send_a[pl.ds(8 * k + j, 32, stride=16), :] = grid[32 * j : 32 * j + 32, 128 * k : 128 * k + 128]
+
+    sides = jnp.where(jnp.logical_and(has_low, has_high), 2, 1)
+    pl.semaphore_wait(barrier, WORKERS - 1 + half + sides)
 
     def to_low(group):
         comps = pl.ds(0, 2) if group == 0 else pl.ds(2, 1)
@@ -255,16 +263,24 @@
     def _():
         to_high(0).start()
 
-    def send(source, target, sems, count, stride, dest):
+    def send(source, target, sems, align, count, from_spot, to_spot, dest):
         return pltpu.make_async_remote_copy(
-            source.at[rows(dest * stride, count)], target.at[rows(me * stride, count)],
+            source.at[rows(to_spot, align, count)], target.at[rows(from_spot, align, count)],
             sems.at[0], sems.at[1], device_id={"gz": plane, "pa": dest})
 
-    def start_a(i, _):
-        send(send_a, recv_a, a_sems, 8, 8, partner(me, i)).start()
-        return 0
-
-    lax.fori_loop(0, RANKS - 1, start_a, 0)
+    def to_workers(source, target, sems, count):
+        def start(i, _):
+            spot = partner(me, i)
+            send(source, target, sems, count, count, me, spot, rank(spot, 0)).start()
+            return 0
+
+        lax.fori_loop(0, WORKERS - 1, start, 0)
+
+        @pl.when(late)
+        def _():
+            send(source, target, sems, count, count, me, place, rank(place, 0)).start()
+
+    to_workers(send_a, recv_a, a_sems, 16)
 
     @pl.when(has_low)
     def _():
@@ -298,16 +314,9 @@
     omega_x = [(-(ky * w[a][1]) - dz_v[a][0], ky * w[a][0] - dz_v[a][1]) for a in range(8)]
     omega_y = [(dz_u[a][0] + kx(a) * w[a][1], dz_u[a][1] - kx(a) * w[a][0]) for a in range(8)]
     grid = x_inverse([omega_x, omega_y], turn_cos, turn_sin, x_in)
-    for j in range(4):
-        send_b[pl.ds(j, 64, stride=4), :] = grid[64 * j : 64 * j + 64]
-
-    def start_b(i, _):
-        send(send_b, recv_b, b_sems, 4, 4, partner(me, i)).start()
-        return 0
-
-    lax.fori_loop(0, RANKS - 1, start_b, 0)
-    recv_a[rows(me * 8, 8), :] = send_a[rows(me * 8, 8), :]
-    recv_b[rows(me * 4, 4), :] = send_b[rows(me * 4, 4), :]
+    for j in range(8):
+        send_b[pl.ds(j, 32, stride=8), :] = grid[32 * j : 32 * j + 32]
+    to_workers(send_b, recv_b, b_sems, 8)
 
     def wait_all(ref, sem, count):
         view = ref.at[pl.ds(0, count)]
@@ -315,49 +324,61 @@
 
     for i in rest:
         load(i).wait()
-    cos, sin = y_turn[0], y_turn[1]
-    wait_all(recv_a, a_sems.at[1], 8 * (RANKS - 1))
-
-    def gathered(ref, stride, base, e):
-        return jnp.concatenate(
-            [ref[pl.ds(base + e, 64, stride=stride), :], ref[pl.ds(base + 2 + e, 64, stride=stride), :]], 0)
-
-    first = y_turned(
-        jnp.concatenate([gathered(recv_a, 8, 4 * k, e) for k in range(2) for e in range(2)], 1), cos, sin, y_in)
-    first = [dot(split(value), y_grid) for value in first]
-    wait_all(recv_b, b_sems.at[1], 4 * (RANKS - 1))
-    second = y_turned(jnp.concatenate([gathered(recv_b, 4, 0, e) for e in range(2)], 1), cos, sin, y_in)
-    second = [dot(split(value), y_grid) for value in second]
-
-    def last(parts):
-        return dot(y_out, split(jnp.concatenate(parts, 1)))
-
-    products = [[], [], []]
-    for e in range(2):
-        uv, wz, xy = first[e], first[2 + e], second[e]
-        uv, vu = uv[:, :128], uv[:, 128:]
-        wz, zw = wz[:, :128], wz[:, 128:]
-        xy, yx = xy[:, :128], xy[:, 128:]
-        products[0].append(vu * zw - wz * yx)
-        products[1].append(wz * xy - uv * zw)
-        products[2].append(uv * yx)
-    for comp in range(3):
-        table = y_diff if comp == 2 else y_low
-        spectral = last([y_forward(value, cos, sin, table) for value in products[comp]])
-        for e in range(2):
-            send_c[pl.ds(2 * comp + e, 64, stride=8), :] = spectral[:, 128 * e : 128 * e + 128]
-
-    def start_c(i, _):
-        dest = partner(me, i)
-
-        @pl.when(dest <= LAST_RANK)
+    inside = me <= LAST_RANK
+
+    @pl.when(worker)
+    def _():
+        recv_a[rows(me, 16, 16), :] = send_a[rows(place, 16, 16), :]
+        recv_b[rows(me, 8, 8), :] = send_b[rows(place, 8, 8), :]
+        cos, sin = y_turn[0], y_turn[1]
+
+        def gathered(ref, stride, base):
+            return jnp.concatenate(
+                [ref[pl.ds(base, 64, stride=stride), :], ref[pl.ds(base + 4, 64, stride=stride), :]], 0)
+
+        def on_grid(ref, stride, bases):
+            turned = y_turned(jnp.concatenate([gathered(ref, stride, base) for base in bases], 1), cos, sin, y_in)
+            return [dot(split(value), y_grid) for value in turned]
+
+        wait_all(recv_a, a_sems.at[1], 16 * (RANKS - 1))
+        first = on_grid(recv_a, 16, [8 * k + e for k in range(2) for e in range(4)])
+        wait_all(recv_b, b_sems.at[1], 8 * (RANKS - 1))
+        second = on_grid(recv_b, 8, range(4))
+
+        products = [[], [], []]
+        for e in range(4):
+            uv, wz, xy = first[e], first[4 + e], second[e]
+            uv, vu = uv[:, :128], uv[:, 128:]
+            wz, zw = wz[:, :128], wz[:, 128:]
+            xy, yx = xy[:, :128], xy[:, 128:]
+            products[0].append(vu * zw - wz * yx)
+            products[1].append(wz * xy - uv * zw)
+            products[2].append(uv * yx)
+        for comp in range(3):
+            table = y_diff if comp == 2 else y_low
+            lines = [y_forward(value, cos, sin, table) for value in products[comp]]
+            spectral = dot(y_out, split(jnp.concatenate(lines, 1)))
+            for e in range(4):
+                send_c[pl.ds(4 * comp + e, 64, stride=16), :] = spectral[:, 128 * e : 128 * e + 128]
+
+        def start_c(spot, to_half):
+            dest = rank(spot, to_half)
+
+            @pl.when(dest <= LAST_RANK)
+            def _():
+                send(send_c, recv_c, c_sems, 16, 12, place, dest, dest).start()
+
+        for to_half in range(2):
+            def start(i, _):
+                start_c(partner(me, i), to_half)
+                return 0
+
+            lax.fori_loop(0, WORKERS - 1, start, 0)
+        start_c(place, 1)
+
+        @pl.when(inside)
         def _():
-            send(send_c, recv_c, c_sems, 6, 8, dest).start()
-
-        return 0
-
-    lax.fori_loop(0, RANKS - 1, start_c, 0)
-    inside = me <= LAST_RANK
+            recv_c[rows(place, 16, 12), :] = send_c[rows(me, 16, 12), :]
 
     @pl.when(has_low)
     def _():
@@ -377,12 +398,18 @@
 
     @pl.when(inside)
     def _():
-        recv_c[rows(me * 8, 6), :] = send_c[rows(me * 8, 6), :]
-        wait_all(recv_c, c_sems.at[1], 6 * (RANKS - 1))
+        @pl.when(worker)
+        def _():
+            wait_all(recv_c, c_sems.at[1], 12 * (WORKERS - 1))
+
+        @pl.when(late)
+        def _():
+            wait_all(recv_c, c_sems.at[1], 12 * WORKERS)
+
         plain_cos = [jnp.broadcast_to(x_turn[0, c], (8, 128)) for c in range(8)]
         plain_sin = [jnp.broadcast_to(x_turn[1, c], (8, 128)) for c in range(8)]
         for comp in range(3):
-            block = jnp.concatenate([recv_c[pl.ds(2 * comp + e, 64, stride=8), :] for e in range(2)], 0)
+            block = jnp.concatenate([recv_c[pl.ds(4 * comp + e, 32, stride=16), :] for e in range(4)], 0)
             for a, pair in enumerate(x_forward(block, plain_cos, plain_sin, x_out)):
                 at = pl.ds(128 * a, 128)
                 keep = mask[:, at].astype(F32) * TIME_STEP
@@ -422,16 +449,25 @@
 
     div[0] = div[0] + 0.5 * (w_high[...] - w_low[...])
 
-    wait_all(send_a, a_sems.at[0], 8 * (RANKS - 1))
-    wait_all(send_b, b_sems.at[0], 4 * (RANKS - 1))
-
-    @pl.when(inside)
-    def _():
-        wait_all(send_c, c_sems.at[0], 6 * LAST_RANK)
-
-    @pl.when(jnp.logical_not(inside))
-    def _():
-        wait_all(send_c, c_sems.at[0], 6 * (LAST_RANK + 1))
+    def all_left(times):
+        wait_all(send_a, a_sems.at[0], 16 * times)
+        wait_all(send_b, b_sems.at[0], 8 * times)
+
+    @pl.when(worker)
+    def _():
+        all_left(WORKERS - 1)
+
+        @pl.when(inside)
+        def _():
+            wait_all(send_c, c_sems.at[0], 12 * LAST_RANK)
+
+        @pl.when(jnp.logical_not(inside))
+        def _():
+            wait_all(send_c, c_sems.at[0], 12 * (LAST_RANK + 1))
+
+    @pl.when(late)
+    def _():
+        all_left(WORKERS)
 
     @pl.when(has_low)
     def _():
@@ -462,9 +498,9 @@
         out_specs=(whole, whole),
         scratch_shapes=[
             *(vmem(operand.shape, operand.dtype) for operand in operands), dma((len(operands),)),
-            vmem((512, 128), F32), vmem((512, 128), F32),
-            vmem((256, 128), F32), vmem((256, 128), F32),
-            vmem((512, 128), F32), vmem((512, 128), F32),
+            vmem((512, 128), F32), vmem((1024, 128), F32),
+            vmem((256, 128), F32), vmem((512, 128), F32),
+            vmem((1024, 128), F32), vmem((512, 128), F32),
             vmem((3, 2, 8, 1024), F32), vmem((3, 2, 8, 1024), F32),
             vmem((2, 8, 1024), F32), vmem((2, 8, 1024), F32), vmem((2, 8, 1024), F32),
             dma((2,)), dma((2,)), dma((2,)),

time: 53.9 us -> 52.9 us (0.981)
  the two profiles are of different devices: /device:TPU:65 before, /device:TPU:1 now
where the time goes in v2:
time: 52.9 us; the launch traced here: 52.8 us
  Pallas kernels  50.8 us (96%)
  local copies, waits for them, and re-layouts  1.31 us (2%)
  between operations  0.64 us (1%)
    pallas_call x1, Pallas kernels, on_device(): pl.pallas_call(kernel, name='substep', out_shape=(vmem((3, 1, 2, 8, 1024)...  50.8 us
    unnamed x2, local copies, waits for them, and re-layouts  1.31 us

profile of v2, /device:TPU:1, one launch (start us, length us, event | category | flops | bytes accessed | tf_op | source)
XLA Modules:
  0.0 52.8 jit_solution(9158179154596309097)
XLA Ops:
  0.6 50.8 %substep.1 = (f32[3,1,2,8,1024]{4,3,2,1,0:T(8,128)S(1)}, f32[1,2,8,1024]{3,2,1,0:T(8,128)S(1)}) custom-call(f32[3,1,2,8,1024]{4,3,2,1,0:T(8,128)} %refs_0_.1, s32[8,1024]{1,0:T(8,128)} %refs_1_.1, bf16[2,256,256]{2,1,0:T(8,128)(2,1)} %constant.18.clone.refs_2_, f32[2,8,1,128]{3,2,1,0:T(1,128)} %constant.19.clone.refs_3_, ...), custom_call_target="tpu_custom_call" | custom-call | tf_op jit(solution)/shard_map/substep/pallas_call | solution.py:490
  51.5 0.7 %copy.15 = f32[3,1,2,8,1024]{4,3,2,1,0:T(8,128)} copy(f32[3,1,2,8,1024]{4,3,2,1,0:T(8,128)S(1)} %get-tuple-element.2) | data formatting | bytes 393216
  52.2 0.6 %copy.16 = f32[1,2,8,1024]{3,2,1,0:T(8,128)} copy(f32[1,2,8,1024]{3,2,1,0:T(8,128)S(1)} %get-tuple-element.3) | data formatting | bytes 131072

commit v3 on v1

v3 whole, which is shorter than its diff:
```python
import math

import jax
import jax.numpy as jnp
import numpy as np
from jax import lax
from jax.experimental import pallas as pl
from jax.experimental.pallas import tpu as pltpu
from jax.sharding import PartitionSpec as P


TWO_PI = 2.0 * math.pi
TIME_STEP = 0.2
VISCOSITY = 0.25
RANKS = 64
LAST_RANK = 42
F32 = jnp.float32
BF16 = jnp.bfloat16


def halves(table):
    table = np.asarray(table, np.float32)
    high = table.astype(jnp.bfloat16)
    low = (table - high.astype(np.float32)).astype(jnp.bfloat16)
    return np.stack([high, low])


def tables():
    index = np.arange
    p, b, c, s, q, r = index(64), index(128), index(8), index(8), index(64), index(128)
    d = (2 * p[None, :] + index(2)[:, None]).reshape(-1)
    angle = TWO_PI / 128.0 * (d[:, None] * b[None, :] % 128)
    cos, sin = np.cos(angle) / 32.0, np.sin(angle) / 32.0
    x_in = np.block([[cos, -sin], [sin, cos]])
    angle = TWO_PI / 1024.0 * (c[:, None] * b[None, :])
    x_turn = np.stack([np.cos(angle), np.sin(angle)]).astype(np.float32).reshape(2, 8, 1, 128)
    angle = TWO_PI / 128.0 * (r[:, None] * q[None, :] % 128)
    cos, sin = np.cos(angle) / 32.0, np.sin(angle) / 32.0
    y_in = np.block([[cos, -sin], [sin, cos]])
    angle = TWO_PI / 1024.0 * (r[:, None] * np.tile(s, 16)[None, :])
    y_turn = np.stack([np.cos(angle), np.sin(angle)]).astype(np.float32)
    angle = TWO_PI / 8.0 * (s[:, None] * s[None, :] % 8)
    cos8, sin8 = np.cos(angle), np.sin(angle)
    eye = np.eye(8)
    real = np.kron(np.eye(2), np.kron(eye, cos8))
    imag = np.kron(np.eye(2), np.kron(eye, -sin8))
    both = np.concatenate([real, imag], 0)
    y_grid = np.concatenate([both, np.roll(both, 64, axis=1)], 1)
    real = np.kron(eye, cos8) / 32.0
    imag = np.kron(eye, -sin8) / 32.0
    line = np.concatenate([real, imag, imag, -real], 1)
    y_low = np.concatenate([line, np.zeros_like(line)], 0)
    y_diff = np.concatenate([line, -line], 0)
    angle = TWO_PI / 128.0 * (q[:, None] * r[None, :] % 128)
    y_out = np.concatenate([np.cos(angle), np.sin(angle)], 1)
    angle = TWO_PI / 128.0 * (d[:, None] * b[None, :] % 128)
    x_out = np.concatenate([np.cos(angle), np.sin(angle)], 1) / 32.0
    return dict(
        x_in=halves(x_in),
        x_turn=x_turn,
        y_in=halves(y_in),
        y_turn=y_turn,
        y_grid=halves(y_grid),
        y_low=halves(y_low),
        y_diff=halves(y_diff),
        y_out=halves(y_out),
        x_out=halves(x_out),
    )


NAMES = ("x_in", "x_turn", "y_in", "y_turn", "y_grid", "y_low", "y_diff", "y_out", "x_out")


def split(value):
    high = value.astype(BF16)
    return high, (value - high.astype(F32)).astype(BF16)


def dot(left, right, contract=((1,), (0,))):
    def one(i, j):
        return lax.dot_general(left[i], right[j], (contract, ((), ())), preferred_element_type=F32)

    return one(0, 0) + (one(0, 1) + one(1, 0))


def eight(values, sign):
    count = len(values)
    if count == 1:
        return values
    even, odd = eight(values[0::2], sign), eight(values[1::2], sign)
    half = count // 2
    low, high = [], []
    for k in range(half):
        (er, ei), (qr, qi) = even[k], odd[k]
        turn = 8 // count * k
        if turn == 0:
            tr, ti = qr, qi
        elif turn == 2:
            tr, ti = -sign * qi, sign * qr
        else:
            root = math.sqrt(0.5)
            if turn == 1:
                tr, ti = root * (qr - sign * qi), root * (qi + sign * qr)
            else:
                tr, ti = -root * (qr + sign * qi), root * (sign * qr - qi)
        low.append((er + tr, ei + ti))
        high.append((er - tr, ei - ti))
    return low + high


def x_inverse(fields, turn_cos, turn_sin, table):
    real, imag = [], []
    for field in fields:
        for c, (vr, vi) in enumerate(eight(field, 1.0)):
            real.append(vr * turn_cos[c] - vi * turn_sin[c])
            imag.append(vr * turn_sin[c] + vi * turn_cos[c])
    lines = jnp.concatenate([jnp.concatenate(real, 0), jnp.concatenate(imag, 0)], 1)
    return dot(table, split(lines), ((1,), (1,)))


def y_turned(modes, cos, sin, table):
    lines = dot(table, split(modes))
    out = []
    for k in range(modes.shape[1] // 128):
        vr, vi = lines[:128, 128 * k : 128 * k + 128], lines[128:, 128 * k : 128 * k + 128]
        out.append(jnp.concatenate([vr * cos - vi * sin, vr * sin + vi * cos], 1))
    return out


def y_forward(product, cos, sin, table):
    line = dot(split(product), table)
    one, two = line[:, :128], line[:, 128:]
    return jnp.concatenate([one * cos + two * sin, two * cos - one * sin], 0)


def x_forward(block, turn_cos, turn_sin, table):
    line = dot(split(block.T), table)
    values = []
    for c in range(8):
        re, im = line[8 * c : 8 * c + 8], line[64 + 8 * c : 72 + 8 * c]
        vr, vi = re[:, :128] + im[:, 128:], im[:, :128] - re[:, 128:]
        values.append((vr * turn_cos[c] + vi * turn_sin[c], vi * turn_cos[c] - vr * turn_sin[c]))
    return eight(values, -1.0)


HOPS = [(dy, dz, dx) for dy in (4, 3, 5, 2, 6, 1, 7, 0) for dx in (2, 1, 3, 0) for dz in (1, 0)][:-1]


def partners(me):
    x, z, y = lax.rem(me, 4), lax.rem(lax.div(me, 4), 2), lax.div(me, 8)
    xs = [lax.rem(x + i, 4) for i in range(4)]
    zs = [4 * lax.rem(z + i, 2) for i in range(2)]
    ys = [8 * lax.rem(y + i, 8) for i in range(8)]
    return [ys[dy] + zs[dz] + xs[dx] for dy, dz, dx in HOPS]


def rows(start, align, count):
    return pl.ds(pl.multiple_of(start * align, align), count)


def kernel(*refs):
    count = 2 + len(NAMES)
    sources, out, div, held = refs[:count], refs[count], refs[count + 1], refs[count + 2 : 2 * count + 2]
    body(sources, held, out, div, *refs[2 * count + 2 :])


def body(sources, held, out, div, load_sems,
           send_a, recv_a, send_w, recv_w, send_c, recv_c, uv_send, uv_low, uv_high,
           low, high, w_low, w_high, w_send, a_sems, hz_sems, c_sems, uv_sems, halo_sems, w_sems):
    me, plane = lax.axis_index("pa"), lax.axis_index("gz")
    barrier = pltpu.get_barrier_semaphore()
    vel, mask, x_in, x_turn, y_in, y_turn, y_grid, y_low, y_diff, y_out, x_out = held

    def load(i):
        return pltpu.make_async_copy(sources[i], held[i], load_sems.at[i])

    for i in (0, 2, 3):
        load(i).start()

    others = partners(me)
    for other in others:
        pl.semaphore_signal(barrier, inc=1, device_id={"gz": plane, "pa": other})
    has_low, has_high = plane > 0, plane < 7

    @pl.when(has_low)
    def _():
        pl.semaphore_signal(barrier, inc=1, device_id={"gz": plane - 1, "pa": me})

    @pl.when(has_high)
    def _():
        pl.semaphore_signal(barrier, inc=1, device_id={"gz": plane + 1, "pa": me})

    rest = [i for i in range(len(held)) if i not in (0, 2, 3)]
    for i in rest:
        load(i).start()
    sub = lax.broadcasted_iota(jnp.int32, (8, 128), 0)
    lane = lax.broadcasted_iota(jnp.int32, (8, 128), 1)
    modes = me * 8 + sub
    ky = (TWO_PI / 1024.0) * modes.astype(F32)
    weight = jnp.where(modes == 0, 1.0, 2.0).astype(F32)

    def kx(a):
        return (TWO_PI / 1024.0) * (lane + (128 * a - 1024 * (a // 4))).astype(F32)

    def piece(ref, *lead):
        return [ref[(*lead, slice(None), pl.ds(128 * a, 128))] for a in range(8)]

    for i in (0, 2, 3):
        load(i).wait()
    turn_cos = [weight * x_turn[0, c] for c in range(8)]
    turn_sin = [weight * x_turn[1, c] for c in range(8)]

    def field(comp):
        return list(zip(piece(vel, comp, 0, 0), piece(vel, comp, 0, 1), strict=True))

    u, v, w = field(0), field(1), field(2)
    omega_z = [
        (ky * u[a][1] - kx(a) * v[a][1], kx(a) * v[a][0] - ky * u[a][0]) for a in range(8)
    ]
    curl_x = [(-(ky * w[a][1]), ky * w[a][0]) for a in range(8)]
    curl_y = [(kx(a) * w[a][1], -(kx(a) * w[a][0])) for a in range(8)]
    grid = x_inverse([u, v, w, omega_z, curl_x, curl_y], turn_cos, turn_sin, x_in)
    for k in range(3):
        for j in range(4):
            send_a[pl.ds(4 * k + j, 64, stride=16), :] = grid[64 * j : 64 * j + 64, 128 * k : 128 * k + 128]

    @pl.when(jnp.logical_and(has_low, has_high))
    def _():
        pl.semaphore_wait(barrier, RANKS + 1)

    @pl.when(jnp.logical_not(jnp.logical_and(has_low, has_high)))
    def _():
        pl.semaphore_wait(barrier, RANKS)

    def send(source, target, sems, align, count, dest):
        return pltpu.make_async_remote_copy(
            source.at[rows(dest, align, count)], target.at[rows(me, align, count)],
            sems.at[0], sems.at[1], device_id={"gz": plane, "pa": dest})

    for other in others:
        send(send_a, recv_a, a_sems, 16, 12, other).start()

    def beside(source, target_low, target_high, sems):
        down = pltpu.make_async_remote_copy(
            source, target_high, sems.at[0], sems.at[1], device_id={"gz": plane - 1, "pa": me})
        up = pltpu.make_async_remote_copy(
            source, target_low, sems.at[2], sems.at[3], device_id={"gz": plane + 1, "pa": me})
        return down, up

    def start_beside(pair):
        @pl.when(has_low)
        def _():
            pair[0].start()

        @pl.when(has_high)
        def _():
            pair[1].start()

    def from_beside(pair):
        @pl.when(has_low)
        def _():
            pair[1].wait_recv()

        @pl.when(has_high)
        def _():
            pair[0].wait_recv()

    def left_beside(pair):
        @pl.when(has_low)
        def _():
            pair[0].wait_send()

        @pl.when(has_high)
        def _():
            pair[1].wait_send()

    halo = beside(vel.at[:, 0], low, high, halo_sems)
    uv_halo = beside(uv_send, uv_low, uv_high, uv_sems)
    w_halo = beside(w_send, w_low, w_high, w_sems)
    start_beside(halo)

    @pl.when(jnp.logical_not(has_low))
    def _():
        low[...] = jnp.zeros_like(low)
        uv_low[...] = jnp.zeros_like(uv_low)
        w_low[...] = jnp.zeros_like(w_low)

    @pl.when(jnp.logical_not(has_high))
    def _():
        high[...] = jnp.zeros_like(high)
        uv_high[...] = jnp.zeros_like(uv_high)
        w_high[...] = jnp.zeros_like(w_high)

    recv_a[rows(me, 16, 12), :] = send_a[rows(me, 16, 12), :]

    def wait_all(ref, sem, count):
        view = ref.at[pl.ds(0, count)]
        pltpu.make_async_copy(view, view, sem).wait()

    for i in rest:
        load(i).wait()
    cos, sin = y_turn[0], y_turn[1]
    wait_all(recv_a, a_sems.at[1], 12 * (RANKS - 1))

    def gathered(base):
        return jnp.concatenate(
            [recv_a[pl.ds(base, 64, stride=16), :], recv_a[pl.ds(base + 2, 64, stride=16), :]], 0)

    def on_grid(pairs):
        turned = y_turned(
            jnp.concatenate([gathered(4 * k + e) for k in pairs for e in range(2)], 1), cos, sin, y_in)
        return [dot(split(value), y_grid) for value in turned]

    fields = on_grid((0,))
    for e in range(2):
        uv_send[e] = fields[e][:, :128]
    start_beside(uv_halo)
    fields = fields + on_grid((1, 2))
    from_beside(uv_halo)

    def last(parts):
        return dot(y_out, split(jnp.concatenate(parts, 1)))

    sign = jnp.where(lax.broadcasted_iota(jnp.int32, (128, 128), 1) < 64, 0.5, -0.5).astype(F32)
    products = [[], [], []]
    for e in range(2):
        uv, wz, xy = fields[e], fields[2 + e], fields[4 + e]
        uv, vu = uv[:, :128], uv[:, 128:]
        wz, zw = wz[:, :128], wz[:, 128:]
        slope = sign * (uv_high[e] - uv_low[e])
        xy, yx = xy[:, :128] + pltpu.roll(slope, 64, 1), xy[:, 128:] + slope
        products[0].append(vu * zw - wz * yx)
        products[1].append(wz * xy - uv * zw)
        products[2].append(uv * yx)

    def spectral(comp):
        table = y_diff if comp == 2 else y_low
        return last([y_forward(value, cos, sin, table) for value in products[comp]])

    def to_inside(source, target, sems, count):
        for other in others:
            @pl.when(other <= LAST_RANK)
            def _(other=other):
                send(source, target, sems, count, count, other).start()

    modes_w = spectral(2)
    for e in range(2):
        send_w[pl.ds(e, 64, stride=2), :] = modes_w[:, 128 * e : 128 * e + 128]
    to_inside(send_w, recv_w, hz_sems, 2)
    for comp in range(2):
        modes_c = spectral(comp)
        for e in range(2):
            send_c[pl.ds(2 * comp + e, 64, stride=4), :] = modes_c[:, 128 * e : 128 * e + 128]
    to_inside(send_c, recv_c, c_sems, 4)

    inside = me <= LAST_RANK

    from_beside(halo)

    for comp in range(3):
        for i in range(2):
            for a in range(8):
                at = pl.ds(128 * a, 128)
                mid = vel[comp, 0, i, :, at]
                viscous = (high[comp, i, :, at] - 2.0 * mid + low[comp, i, :, at]) - (kx(a) * kx(a) + ky * ky) * mid
                out[comp, 0, i, :, at] = mid + (TIME_STEP * VISCOSITY) * viscous

    plain_cos = [jnp.broadcast_to(x_turn[0, c], (8, 128)) for c in range(8)]
    plain_sin = [jnp.broadcast_to(x_turn[1, c], (8, 128)) for c in range(8)]

    def add_nonlinear(comp, ref, base, stride):
        block = jnp.concatenate([ref[pl.ds(base + e, 64, stride=stride), :] for e in range(2)], 0)
        for a, pair in enumerate(x_forward(block, plain_cos, plain_sin, x_out)):
            at = pl.ds(128 * a, 128)
            keep = mask[:, at].astype(F32) * TIME_STEP
            for i in range(2):
                out[comp, 0, i, :, at] = out[comp, 0, i, :, at] + pair[i] * keep

    @pl.when(inside)
    def _():
        recv_w[rows(me, 2, 2), :] = send_w[rows(me, 2, 2), :]
        recv_c[rows(me, 4, 4), :] = send_c[rows(me, 4, 4), :]
        wait_all(recv_w, hz_sems.at[1], 2 * (RANKS - 1))
        add_nonlinear(2, recv_w, 0, 2)

    w_send[...] = out[2, 0]
    start_beside(w_halo)

    @pl.when(inside)
    def _():
        wait_all(recv_c, c_sems.at[1], 4 * (RANKS - 1))
        add_nonlinear(0, recv_c, 0, 4)
        add_nonlinear(1, recv_c, 2, 4)

    for a in range(8):
        at = pl.ds(128 * a, 128)
        div[0, 0, :, at] = -(kx(a) * out[0, 0, 1, :, at]) - ky * out[1, 0, 1, :, at]
        div[0, 1, :, at] = kx(a) * out[0, 0, 0, :, at] + ky * out[1, 0, 0, :, at]

    from_beside(w_halo)
    div[0] = div[0] + 0.5 * (w_high[...] - w_low[...])

    wait_all(send_a, a_sems.at[0], 12 * (RANKS - 1))

    @pl.when(inside)
    def _():
        wait_all(send_w, hz_sems.at[0], 2 * LAST_RANK)
        wait_all(send_c, c_sems.at[0], 4 * LAST_RANK)

    @pl.when(jnp.logical_not(inside))
    def _():
        wait_all(send_w, hz_sems.at[0], 2 * (LAST_RANK + 1))
        wait_all(send_c, c_sems.at[0], 4 * (LAST_RANK + 1))

    for pair in (halo, uv_halo, w_halo):
        left_beside(pair)


def on_device(velocity, mode_mask):
    constants = tables()
    operands = (velocity, mode_mask, *(jnp.asarray(constants[name]) for name in NAMES))
    whole = pl.BlockSpec(memory_space=pltpu.VMEM)
    dma, vmem = pltpu.SemaphoreType.DMA, pltpu.VMEM
    return pl.pallas_call(
        kernel,
        name="substep",
        out_shape=(
            vmem((3, 1, 2, 8, 1024), F32),
            vmem((1, 2, 8, 1024), F32),
        ),
        in_specs=[pl.BlockSpec(memory_space=pl.ANY)] * len(operands),
        out_specs=(whole, whole),
        scratch_shapes=[
            *(vmem(operand.shape, operand.dtype) for operand in operands), dma((len(operands),)),
            vmem((1024, 128), F32), vmem((1024, 128), F32),
            vmem((128, 128), F32), vmem((128, 128), F32),
            vmem((256, 128), F32), vmem((256, 128), F32),
            *[vmem((2, 128, 128), F32)] * 3,
            *[vmem((3, 2, 8, 1024), F32)] * 2,
            *[vmem((2, 8, 1024), F32)] * 3,
            *[dma((2,))] * 3, *[dma((4,))] * 3,
        ],
        compiler_params=pltpu.CompilerParams(collective_id=0, has_side_effects=True),
    )(*operands)


def solution(mesh):
    return jax.shard_map(
        on_device,
        mesh=mesh,
        in_specs=(P(None, "gz", None, "pa", None), P("pa", None)),
        out_specs=(P(None, "gz", None, "pa", None), P("gz", None, "pa", None)),
        check_vma=False,
    )
```

time: 53.9 us -> 48.9 us (0.907)
  the two profiles are of different devices: /device:TPU:65 before, /device:TPU:1 now
where the time goes in v3:
time: 48.9 us; the launch traced here: 48.8 us
  Pallas kernels  46.8 us (96%)
  local copies, waits for them, and re-layouts  1.31 us (3%)
  between operations  0.64 us (1%)
    pallas_call x1, Pallas kernels, on_device(): pl.pallas_call(kernel, name='substep', out_shape=(vmem((3, 1, 2, 8, 1024)...  46.8 us
    unnamed x2, local copies, waits for them, and re-layouts  1.31 us

profile of v3, /device:TPU:1, one launch (start us, length us, event | category | flops | bytes accessed | tf_op | source)
XLA Modules:
  0.0 48.8 jit_solution(17499656229293955297)
XLA Ops:
  0.6 46.8 %substep.1 = (f32[3,1,2,8,1024]{4,3,2,1,0:T(8,128)S(1)}, f32[1,2,8,1024]{3,2,1,0:T(8,128)S(1)}) custom-call(f32[3,1,2,8,1024]{4,3,2,1,0:T(8,128)} %refs_0_.1, s32[8,1024]{1,0:T(8,128)} %refs_1_.1, bf16[2,256,256]{2,1,0:T(8,128)(2,1)} %constant.18.clone.refs_2_, f32[2,8,1,128]{3,2,1,0:T(1,128)} %constant.19.clone.refs_3_, ...), custom_call_target="tpu_custom_call" | custom-call | tf_op jit(solution)/shard_map/substep/pallas_call | solution.py:424
  47.5 0.7 %copy.15 = f32[3,1,2,8,1024]{4,3,2,1,0:T(8,128)} copy(f32[3,1,2,8,1024]{4,3,2,1,0:T(8,128)S(1)} %get-tuple-element.2) | data formatting | bytes 393216
  48.2 0.6 %copy.16 = f32[1,2,8,1024]{3,2,1,0:T(8,128)} copy(f32[1,2,8,1024]{3,2,1,0:T(8,128)S(1)} %get-tuple-element.3) | data formatting | bytes 131072

commit v4 on v3

--- a/solution.py
+++ b/solution.py
@@ -143,7 +143,7 @@
     return eight(values, -1.0)
 
 
-HOPS = [(dy, dz, dx) for dy in (4, 3, 5, 2, 6, 1, 7, 0) for dx in (2, 1, 3, 0) for dz in (1, 0)][:-1]
+HOPS = [(dy, dz, dx) for dz in (1, 0) for dy in (4, 3, 5, 2, 6, 1, 7, 0) for dx in (2, 1, 3, 0)][:-1]
 
 
 def partners(me):
@@ -165,8 +165,8 @@
 
 
 def body(sources, held, out, div, load_sems,
-           send_a, recv_a, send_w, recv_w, send_c, recv_c, uv_send, uv_low, uv_high,
-           low, high, w_low, w_high, w_send, a_sems, hz_sems, c_sems, uv_sems, halo_sems, w_sems):
+           send_u, recv_u, send_a, recv_a, send_w, recv_w, send_c, recv_c, uv_send, uv_low, uv_high,
+           low, high, w_low, w_high, w_send, u_sems, a_sems, hz_sems, c_sems, uv_sems, halo_sems, w_sems):
     me, plane = lax.axis_index("pa"), lax.axis_index("gz")
     barrier = pltpu.get_barrier_semaphore()
     vel, mask, x_in, x_turn, y_in, y_turn, y_grid, y_low, y_diff, y_out, x_out = held
@@ -217,12 +217,15 @@
     omega_z = [
         (ky * u[a][1] - kx(a) * v[a][1], kx(a) * v[a][0] - ky * u[a][0]) for a in range(8)
     ]
-    curl_x = [(-(ky * w[a][1]), ky * w[a][0]) for a in range(8)]
     curl_y = [(kx(a) * w[a][1], -(kx(a) * w[a][0])) for a in range(8)]
-    grid = x_inverse([u, v, w, omega_z, curl_x, curl_y], turn_cos, turn_sin, x_in)
-    for k in range(3):
-        for j in range(4):
-            send_a[pl.ds(4 * k + j, 64, stride=16), :] = grid[64 * j : 64 * j + 64, 128 * k : 128 * k + 128]
+    grid = x_inverse([u, v, w, omega_z, curl_y, curl_y], turn_cos, turn_sin, x_in)
+    left = lax.broadcasted_iota(jnp.int32, (64, 128), 1) < 64
+    for j in range(4):
+        send_u[pl.ds(j, 64, stride=4), :] = grid[64 * j : 64 * j + 64, :128]
+        send_a[pl.ds(j, 64, stride=8), :] = grid[64 * j : 64 * j + 64, 128:256]
+    for ri in range(2):
+        first, second = (grid[128 * ri + 64 * e : 128 * ri + 64 * e + 64, 256:] for e in range(2))
+        send_a[pl.ds(4 + ri, 64, stride=8), :] = jnp.where(left, second, first)
 
     @pl.when(jnp.logical_and(has_low, has_high))
     def _():
@@ -238,7 +241,9 @@
             sems.at[0], sems.at[1], device_id={"gz": plane, "pa": dest})
 
     for other in others:
-        send(send_a, recv_a, a_sems, 16, 12, other).start()
+        send(send_u, recv_u, u_sems, 4, 4, other).start()
+    for other in others:
+        send(send_a, recv_a, a_sems, 8, 6, other).start()
 
     def beside(source, target_low, target_high, sems):
         down = pltpu.make_async_remote_copy(
@@ -277,7 +282,6 @@
     halo = beside(vel.at[:, 0], low, high, halo_sems)
     uv_halo = beside(uv_send, uv_low, uv_high, uv_sems)
     w_halo = beside(w_send, w_low, w_high, w_sems)
-    start_beside(halo)
 
     @pl.when(jnp.logical_not(has_low))
     def _():
@@ -291,7 +295,8 @@
         uv_high[...] = jnp.zeros_like(uv_high)
         w_high[...] = jnp.zeros_like(w_high)
 
-    recv_a[rows(me, 16, 12), :] = send_a[rows(me, 16, 12), :]
+    recv_u[rows(me, 4, 4), :] = send_u[rows(me, 4, 4), :]
+    recv_a[rows(me, 8, 6), :] = send_a[rows(me, 8, 6), :]
 
     def wait_all(ref, sem, count):
         view = ref.at[pl.ds(0, count)]
@@ -300,22 +305,28 @@
     for i in rest:
         load(i).wait()
     cos, sin = y_turn[0], y_turn[1]
-    wait_all(recv_a, a_sems.at[1], 12 * (RANKS - 1))
-
-    def gathered(base):
-        return jnp.concatenate(
-            [recv_a[pl.ds(base, 64, stride=16), :], recv_a[pl.ds(base + 2, 64, stride=16), :]], 0)
-
-    def on_grid(pairs):
-        turned = y_turned(
-            jnp.concatenate([gathered(4 * k + e) for k in pairs for e in range(2)], 1), cos, sin, y_in)
+    def gathered(ref, stride, e):
+        return jnp.concatenate([ref[pl.ds(e, 64, stride=stride), :], ref[pl.ds(e + 2, 64, stride=stride), :]], 0)
+
+    def on_grid(blocks):
+        turned = y_turned(jnp.concatenate(blocks, 1), cos, sin, y_in)
         return [dot(split(value), y_grid) for value in turned]
 
-    fields = on_grid((0,))
+    wait_all(recv_u, u_sems.at[1], 4 * (RANKS - 1))
+    fields = on_grid([gathered(recv_u, 4, e) for e in range(2)])
     for e in range(2):
         uv_send[e] = fields[e][:, :128]
     start_beside(uv_halo)
-    fields = fields + on_grid((1, 2))
+    start_beside(halo)
+    wait_all(recv_a, a_sems.at[1], 6 * (RANKS - 1))
+    row, col = (lax.broadcasted_iota(jnp.int32, (64, 128), i) for i in range(2))
+    ky_grid = (TWO_PI / 1024.0) * (8 * row + lax.rem(col, 8)).astype(F32)
+    blocks = [gathered(recv_a, 8, e) for e in range(2)]
+    curl_re, curl_im = recv_a[pl.ds(4, 64, stride=8), :], recv_a[pl.ds(5, 64, stride=8), :]
+    one, two = blocks[0], pltpu.roll(blocks[1], 64, 1)
+    pair_one = [jnp.where(left, -(ky_grid * one[64:]), curl_re), jnp.where(left, ky_grid * one[:64], curl_im)]
+    pair_two = [jnp.where(left, curl_re, -(ky_grid * two[64:])), jnp.where(left, curl_im, ky_grid * two[:64])]
+    fields = fields + on_grid([*blocks, jnp.concatenate(pair_one, 0), jnp.concatenate(pair_two, 0)])
     from_beside(uv_halo)
 
     def last(parts):
@@ -328,7 +339,8 @@
         uv, vu = uv[:, :128], uv[:, 128:]
         wz, zw = wz[:, :128], wz[:, 128:]
         slope = sign * (uv_high[e] - uv_low[e])
-        xy, yx = xy[:, :128] + pltpu.roll(slope, 64, 1), xy[:, 128:] + slope
+        xy, yx = (xy[:, :128], xy[:, 128:]) if e == 0 else (xy[:, 128:], xy[:, :128])
+        xy, yx = xy + pltpu.roll(slope, 64, 1), yx + slope
         products[0].append(vu * zw - wz * yx)
         products[1].append(wz * xy - uv * zw)
         products[2].append(uv * yx)
@@ -400,7 +412,8 @@
     from_beside(w_halo)
     div[0] = div[0] + 0.5 * (w_high[...] - w_low[...])
 
-    wait_all(send_a, a_sems.at[0], 12 * (RANKS - 1))
+    wait_all(send_u, u_sems.at[0], 4 * (RANKS - 1))
+    wait_all(send_a, a_sems.at[0], 6 * (RANKS - 1))
 
     @pl.when(inside)
     def _():
@@ -432,13 +445,14 @@
         out_specs=(whole, whole),
         scratch_shapes=[
             *(vmem(operand.shape, operand.dtype) for operand in operands), dma((len(operands),)),
-            vmem((1024, 128), F32), vmem((1024, 128), F32),
+            vmem((256, 128), F32), vmem((256, 128), F32),
+            vmem((512, 128), F32), vmem((512, 128), F32),
             vmem((128, 128), F32), vmem((128, 128), F32),
             vmem((256, 128), F32), vmem((256, 128), F32),
             *[vmem((2, 128, 128), F32)] * 3,
             *[vmem((3, 2, 8, 1024), F32)] * 2,
             *[vmem((2, 8, 1024), F32)] * 3,
-            *[dma((2,))] * 3, *[dma((4,))] * 3,
+            *[dma((2,))] * 4, *[dma((4,))] * 3,
         ],
         compiler_params=pltpu.CompilerParams(collective_id=0, has_side_effects=True),
     )(*operands)

time: 48.9 us -> 46.3 us (0.947)
  the two profiles are of different devices: /device:TPU:1 before, /device:TPU:65 now
where the time goes in v4:
time: 46.3 us; the launch traced here: 46.2 us
  Pallas kernels  44.3 us (96%)
  local copies, waits for them, and re-layouts  1.31 us (3%)
  between operations  0.64 us (1%)
    pallas_call x1, Pallas kernels, on_device(): pl.pallas_call(kernel, name='substep', out_shape=(vmem((3, 1, 2, 8, 1024)...  44.3 us
    unnamed x2, local copies, waits for them, and re-layouts  1.31 us

profile of v4, /device:TPU:65, one launch (start us, length us, event | category | flops | bytes accessed | tf_op | source)
XLA Modules:
  0.0 46.2 jit_solution(17652509586248842464)
XLA Ops:
  0.6 44.3 %substep.1 = (f32[3,1,2,8,1024]{4,3,2,1,0:T(8,128)S(1)}, f32[1,2,8,1024]{3,2,1,0:T(8,128)S(1)}) custom-call(f32[3,1,2,8,1024]{4,3,2,1,0:T(8,128)} %refs_0_.1, s32[8,1024]{1,0:T(8,128)} %refs_1_.1, bf16[2,256,256]{2,1,0:T(8,128)(2,1)} %constant.18.clone.refs_2_, f32[2,8,1,128]{3,2,1,0:T(1,128)} %constant.19.clone.refs_3_, ...), custom_call_target="tpu_custom_call" | custom-call | tf_op jit(solution)/shard_map/substep/pallas_call | solution.py:437
  44.9 0.7 %copy.15 = f32[3,1,2,8,1024]{4,3,2,1,0:T(8,128)} copy(f32[3,1,2,8,1024]{4,3,2,1,0:T(8,128)S(1)} %get-tuple-element.2) | data formatting | bytes 393216
  45.6 0.6 %copy.16 = f32[1,2,8,1024]{3,2,1,0:T(8,128)} copy(f32[1,2,8,1024]{3,2,1,0:T(8,128)S(1)} %get-tuple-element.3) | data formatting | bytes 131072

commit v5 on v4

--- a/solution.py
+++ b/solution.py
@@ -143,7 +143,15 @@
     return eight(values, -1.0)
 
 
-HOPS = [(dy, dz, dx) for dz in (1, 0) for dy in (4, 3, 5, 2, 6, 1, 7, 0) for dx in (2, 1, 3, 0)][:-1]
+HOPS = [(dy, dz, dx) for dz in (1, 0) for dy in (4, 5, 3, 6, 2, 7, 1, 0) for dx in (2, 3, 1, 0)][:-1]
+
+
+def hops(hop):
+    dy, dz, dx = hop
+    return min(dy, 8 - dy) + 4 * dz + min(dx, 4 - dx)
+
+
+FAR = sorted(range(63), key=lambda i: -hops(HOPS[i]))
 
 
 def partners(me):
@@ -174,11 +182,8 @@
     def load(i):
         return pltpu.make_async_copy(sources[i], held[i], load_sems.at[i])
 
-    for i in (0, 2, 3):
-        load(i).start()
-
     others = partners(me)
-    for other in others:
+    for other in (others[i] for i in FAR):
         pl.semaphore_signal(barrier, inc=1, device_id={"gz": plane, "pa": other})
     has_low, has_high = plane > 0, plane < 7
 
@@ -191,7 +196,7 @@
         pl.semaphore_signal(barrier, inc=1, device_id={"gz": plane + 1, "pa": me})
 
     rest = [i for i in range(len(held)) if i not in (0, 2, 3)]
-    for i in rest:
+    for i in (0, 2, 3, *rest):
         load(i).start()
     sub = lax.broadcasted_iota(jnp.int32, (8, 128), 0)
     lane = lax.broadcasted_iota(jnp.int32, (8, 128), 1)
@@ -317,8 +322,8 @@
     for e in range(2):
         uv_send[e] = fields[e][:, :128]
     start_beside(uv_halo)
+    wait_all(recv_a, a_sems.at[1], 6 * (RANKS - 1))
     start_beside(halo)
-    wait_all(recv_a, a_sems.at[1], 6 * (RANKS - 1))
     row, col = (lax.broadcasted_iota(jnp.int32, (64, 128), i) for i in range(2))
     ky_grid = (TWO_PI / 1024.0) * (8 * row + lax.rem(col, 8)).astype(F32)
     blocks = [gathered(recv_a, 8, e) for e in range(2)]
@@ -350,7 +355,7 @@
         return last([y_forward(value, cos, sin, table) for value in products[comp]])
 
     def to_inside(source, target, sems, count):
-        for other in others:
+        for other in (others[i] for i in FAR):
             @pl.when(other <= LAST_RANK)
             def _(other=other):
                 send(source, target, sems, count, count, other).start()
@@ -429,12 +434,23 @@
         left_beside(pair)
 
 
+def store(following, divergence, out, div, sems):
+    copies = [
+        pltpu.make_async_copy(following, out, sems.at[0]),
+        pltpu.make_async_copy(divergence, div, sems.at[1]),
+    ]
+    for copy in copies:
+        copy.start()
+    for copy in copies:
+        copy.wait()
+
+
 def on_device(velocity, mode_mask):
     constants = tables()
     operands = (velocity, mode_mask, *(jnp.asarray(constants[name]) for name in NAMES))
     whole = pl.BlockSpec(memory_space=pltpu.VMEM)
     dma, vmem = pltpu.SemaphoreType.DMA, pltpu.VMEM
-    return pl.pallas_call(
+    held = pl.pallas_call(
         kernel,
         name="substep",
         out_shape=(
@@ -456,6 +472,17 @@
         ],
         compiler_params=pltpu.CompilerParams(collective_id=0, has_side_effects=True),
     )(*operands)
+    return pl.pallas_call(
+        store,
+        name="store",
+        out_shape=(
+            jax.ShapeDtypeStruct((3, 1, 2, 8, 1024), F32),
+            jax.ShapeDtypeStruct((1, 2, 8, 1024), F32),
+        ),
+        in_specs=[whole, whole],
+        out_specs=[pl.BlockSpec(memory_space=pl.ANY)] * 2,
+        scratch_shapes=[dma((2,))],
+    )(*(pltpu.with_memory_space_constraint(value, pltpu.VMEM) for value in held))
 
 
 def solution(mesh):

time: 46.3 us -> 45 us (0.972)
  the two profiles are of different devices: /device:TPU:65 before, /device:TPU:1 now
where the time goes in v5:
time: 45 us; the launch traced here: 44.3 us
  Pallas kernels  43.6 us (97%)
  between operations  0.64 us (1%)
    pallas_call x1, Pallas kernels, on_device(): pl.pallas_call(kernel, name='substep', out_shape=(vmem((3, 1, 2, 8, 1024)...  42.9 us

profile of v5, /device:TPU:1, one launch (start us, length us, event | category | flops | bytes accessed | tf_op | source)
XLA Modules:
  0.0 44.3 jit_solution(17591043526238058598)
XLA Ops:
  0.6 42.9 %substep.1 = (f32[3,1,2,8,1024]{4,3,2,1,0:T(8,128)S(1)}, f32[1,2,8,1024]{3,2,1,0:T(8,128)S(1)}) custom-call(f32[3,1,2,8,1024]{4,3,2,1,0:T(8,128)} %refs_0_.1, s32[8,1024]{1,0:T(8,128)} %refs_1_.1, bf16[2,256,256]{2,1,0:T(8,128)(2,1)} %constant.18.clone.refs_2_, f32[2,8,1,128]{3,2,1,0:T(1,128)} %constant.19.clone.refs_3_, ...), custom_call_target="tpu_custom_call" | custom-call | tf_op jit(solution)/shard_map/substep/pallas_call | solution.py:453
  43.5 0.7 %store.1 = (f32[3,1,2,8,1024]{4,3,2,1,0:T(8,128)}, f32[1,2,8,1024]{3,2,1,0:T(8,128)}) custom-call(f32[3,1,2,8,1024]{4,3,2,1,0:T(8,128)S(1)} %get-tuple-element.4.following, f32[1,2,8,1024]{3,2,1,0:T(8,128)S(1)} %get-tuple-element.5.divergence), custom_call_target="tpu_custom_call" | custom-call | tf_op jit(solution)/shard_map/store/pallas_call | solution.py:475

commit v6 on v5

--- a/solution.py
+++ b/solution.py
@@ -285,7 +285,7 @@
             pair[1].wait_send()
 
     halo = beside(vel.at[:, 0], low, high, halo_sems)
-    uv_halo = beside(uv_send, uv_low, uv_high, uv_sems)
+    uv_halo = [beside(uv_send.at[e], uv_low.at[e], uv_high.at[e], uv_sems.at[e]) for e in range(2)]
     w_halo = beside(w_send, w_low, w_high, w_sems)
 
     @pl.when(jnp.logical_not(has_low))
@@ -318,10 +318,11 @@
         return [dot(split(value), y_grid) for value in turned]
 
     wait_all(recv_u, u_sems.at[1], 4 * (RANKS - 1))
-    fields = on_grid([gathered(recv_u, 4, e) for e in range(2)])
+    fields = []
     for e in range(2):
+        fields += on_grid([gathered(recv_u, 4, e)])
         uv_send[e] = fields[e][:, :128]
-    start_beside(uv_halo)
+        start_beside(uv_halo[e])
     wait_all(recv_a, a_sems.at[1], 6 * (RANKS - 1))
     start_beside(halo)
     row, col = (lax.broadcasted_iota(jnp.int32, (64, 128), i) for i in range(2))
@@ -332,7 +333,8 @@
     pair_one = [jnp.where(left, -(ky_grid * one[64:]), curl_re), jnp.where(left, ky_grid * one[:64], curl_im)]
     pair_two = [jnp.where(left, curl_re, -(ky_grid * two[64:])), jnp.where(left, curl_im, ky_grid * two[:64])]
     fields = fields + on_grid([*blocks, jnp.concatenate(pair_one, 0), jnp.concatenate(pair_two, 0)])
-    from_beside(uv_halo)
+    for pair in uv_halo:
+        from_beside(pair)
 
     def last(parts):
         return dot(y_out, split(jnp.concatenate(parts, 1)))
@@ -430,7 +432,7 @@
         wait_all(send_w, hz_sems.at[0], 2 * (LAST_RANK + 1))
         wait_all(send_c, c_sems.at[0], 4 * (LAST_RANK + 1))
 
-    for pair in (halo, uv_halo, w_halo):
+    for pair in (halo, *uv_halo, w_halo):
         left_beside(pair)
 
 
@@ -468,7 +470,7 @@
             *[vmem((2, 128, 128), F32)] * 3,
             *[vmem((3, 2, 8, 1024), F32)] * 2,
             *[vmem((2, 8, 1024), F32)] * 3,
-            *[dma((2,))] * 4, *[dma((4,))] * 3,
+            *[dma((2,))] * 4, dma((2, 4)), *[dma((4,))] * 2,
         ],
         compiler_params=pltpu.CompilerParams(collective_id=0, has_side_effects=True),
     )(*operands)

time: 45 us -> 44.8 us (level)
  no operation moved by 1% of the time
where the time goes in v6:
time: 44.8 us; the launch traced here: 44.4 us
  Pallas kernels  43.8 us (98%)
  between operations  0.64 us (1%)
    pallas_call x1, Pallas kernels, on_device(): pl.pallas_call(kernel, name='substep', out_shape=(vmem((3, 1, 2, 8, 1024)...  43 us

profile of v6, /device:TPU:1, one launch (start us, length us, event | category | flops | bytes accessed | tf_op | source)
XLA Modules:
  0.0 44.4 jit_solution(3338805606741188267)
XLA Ops:
  0.6 43.0 %substep.1 = (f32[3,1,2,8,1024]{4,3,2,1,0:T(8,128)S(1)}, f32[1,2,8,1024]{3,2,1,0:T(8,128)S(1)}) custom-call(f32[3,1,2,8,1024]{4,3,2,1,0:T(8,128)} %refs_0_.1, s32[8,1024]{1,0:T(8,128)} %refs_1_.1, bf16[2,256,256]{2,1,0:T(8,128)(2,1)} %constant.18.clone.refs_2_, f32[2,8,1,128]{3,2,1,0:T(1,128)} %constant.19.clone.refs_3_, ...), custom_call_target="tpu_custom_call" | custom-call | tf_op jit(solution)/shard_map/substep/pallas_call | solution.py:455
  43.7 0.7 %store.1 = (f32[3,1,2,8,1024]{4,3,2,1,0:T(8,128)}, f32[1,2,8,1024]{3,2,1,0:T(8,128)}) custom-call(f32[3,1,2,8,1024]{4,3,2,1,0:T(8,128)S(1)} %get-tuple-element.4.following, f32[1,2,8,1024]{3,2,1,0:T(8,128)S(1)} %get-tuple-element.5.divergence), custom_call_target="tpu_custom_call" | custom-call | tf_op jit(solution)/shard_map/store/pallas_call | solution.py:477

commit v7 on v6

--- a/solution.py
+++ b/solution.py
@@ -60,15 +60,12 @@
         x_turn=x_turn,
         y_in=halves(y_in),
         y_turn=y_turn,
-        y_grid=halves(y_grid),
-        y_low=halves(y_low),
-        y_diff=halves(y_diff),
-        y_out=halves(y_out),
-        x_out=halves(x_out),
+        late=halves(np.concatenate([y_grid, y_low, y_diff, y_out, x_out], 0)),
     )
 
 
-NAMES = ("x_in", "x_turn", "y_in", "y_turn", "y_grid", "y_low", "y_diff", "y_out", "x_out")
+NAMES = ("x_in", "x_turn", "y_in", "y_turn", "late")
+LATE = ((0, 256), (256, 128), (384, 128), (512, 64), (576, 128))
 
 
 def split(value):
@@ -144,6 +141,7 @@
 
 
 HOPS = [(dy, dz, dx) for dz in (1, 0) for dy in (4, 5, 3, 6, 2, 7, 1, 0) for dx in (2, 3, 1, 0)][:-1]
+HOPS.sort(key=lambda hop: (-hop[1], -min(hop[0], 8 - hop[0]) - min(hop[2], 4 - hop[2])))
 
 
 def hops(hop):
@@ -174,10 +172,11 @@
 
 def body(sources, held, out, div, load_sems,
            send_u, recv_u, send_a, recv_a, send_w, recv_w, send_c, recv_c, uv_send, uv_low, uv_high,
-           low, high, w_low, w_high, w_send, u_sems, a_sems, hz_sems, c_sems, uv_sems, halo_sems, w_sems):
+           low, high, w_low, w_high, u_sems, a_sems, hz_sems, c_sems, uv_sems, halo_sems, w_sems):
     me, plane = lax.axis_index("pa"), lax.axis_index("gz")
     barrier = pltpu.get_barrier_semaphore()
-    vel, mask, x_in, x_turn, y_in, y_turn, y_grid, y_low, y_diff, y_out, x_out = held
+    vel, mask, x_in, x_turn, y_in, y_turn, late_tables = held
+    y_grid, y_low, y_diff, y_out, x_out = (late_tables.at[:, pl.ds(at, size)] for at, size in LATE)
 
     def load(i):
         return pltpu.make_async_copy(sources[i], held[i], load_sems.at[i])
@@ -286,7 +285,7 @@
 
     halo = beside(vel.at[:, 0], low, high, halo_sems)
     uv_halo = [beside(uv_send.at[e], uv_low.at[e], uv_high.at[e], uv_sems.at[e]) for e in range(2)]
-    w_halo = beside(w_send, w_low, w_high, w_sems)
+    w_halo = beside(out.at[2, 0], w_low, w_high, w_sems)
 
     @pl.when(jnp.logical_not(has_low))
     def _():
@@ -402,7 +401,6 @@
         wait_all(recv_w, hz_sems.at[1], 2 * (RANKS - 1))
         add_nonlinear(2, recv_w, 0, 2)
 
-    w_send[...] = out[2, 0]
     start_beside(w_halo)
 
     @pl.when(inside)
@@ -469,7 +467,7 @@
             vmem((256, 128), F32), vmem((256, 128), F32),
             *[vmem((2, 128, 128), F32)] * 3,
             *[vmem((3, 2, 8, 1024), F32)] * 2,
-            *[vmem((2, 8, 1024), F32)] * 3,
+            *[vmem((2, 8, 1024), F32)] * 2,
             *[dma((2,))] * 4, dma((2, 4)), *[dma((4,))] * 2,
         ],
         compiler_params=pltpu.CompilerParams(collective_id=0, has_side_effects=True),

time: 44.8 us -> 44.8 us (level)
  no operation moved by 1% of the time
where the time goes in v7:
time: 44.8 us; the launch traced here: 44.4 us
  Pallas kernels  43.7 us (98%)
  between operations  0.64 us (1%)
    pallas_call x1, Pallas kernels, on_device(): pl.pallas_call(kernel, name='substep', out_shape=(vmem((3, 1, 2, 8, 1024)...  43 us

profile of v7, /device:TPU:1, one launch (start us, length us, event | category | flops | bytes accessed | tf_op | source)
XLA Modules:
  0.0 44.4 jit_solution(6500342264484401699)
XLA Ops:
  0.6 43.0 %substep.1 = (f32[3,1,2,8,1024]{4,3,2,1,0:T(8,128)S(1)}, f32[1,2,8,1024]{3,2,1,0:T(8,128)S(1)}) custom-call(f32[3,1,2,8,1024]{4,3,2,1,0:T(8,128)} %refs_0_.1, s32[8,1024]{1,0:T(8,128)} %refs_1_.1, bf16[2,256,256]{2,1,0:T(8,128)(2,1)} %constant.10.clone.refs_2_, f32[2,8,1,128]{3,2,1,0:T(1,128)} %constant.11.clone.refs_3_, ...), custom_call_target="tpu_custom_call" | custom-call | tf_op jit(solution)/shard_map/substep/pallas_call | solution.py:453
  43.7 0.7 %store.1 = (f32[3,1,2,8,1024]{4,3,2,1,0:T(8,128)}, f32[1,2,8,1024]{3,2,1,0:T(8,128)}) custom-call(f32[3,1,2,8,1024]{4,3,2,1,0:T(8,128)S(1)} %get-tuple-element.4.following, f32[1,2,8,1024]{3,2,1,0:T(8,128)S(1)} %get-tuple-element.5.divergence), custom_call_target="tpu_custom_call" | custom-call | tf_op jit(solution)/shard_map/store/pallas_call | solution.py:475

commit v8 on v7

--- a/solution.py
+++ b/solution.py
@@ -322,8 +322,8 @@
         fields += on_grid([gathered(recv_u, 4, e)])
         uv_send[e] = fields[e][:, :128]
         start_beside(uv_halo[e])
+    start_beside(halo)
     wait_all(recv_a, a_sems.at[1], 6 * (RANKS - 1))
-    start_beside(halo)
     row, col = (lax.broadcasted_iota(jnp.int32, (64, 128), i) for i in range(2))
     ky_grid = (TWO_PI / 1024.0) * (8 * row + lax.rem(col, 8)).astype(F32)
     blocks = [gathered(recv_a, 8, e) for e in range(2)]

time: 44.8 us -> 44.8 us (level)
  no operation moved by 1% of the time
where the time goes in v8:
time: 44.8 us; the launch traced here: 44.4 us
  Pallas kernels  43.7 us (98%)
  between operations  0.64 us (1%)
    pallas_call x1, Pallas kernels, on_device(): pl.pallas_call(kernel, name='substep', out_shape=(vmem((3, 1, 2, 8, 1024)...  43 us

profile of v8, /device:TPU:1, one launch (start us, length us, event | category | flops | bytes accessed | tf_op | source)
XLA Modules:
  0.0 44.4 jit_solution(5695527066044231837)
XLA Ops:
  0.6 43.0 %substep.1 = (f32[3,1,2,8,1024]{4,3,2,1,0:T(8,128)S(1)}, f32[1,2,8,1024]{3,2,1,0:T(8,128)S(1)}) custom-call(f32[3,1,2,8,1024]{4,3,2,1,0:T(8,128)} %refs_0_.1, s32[8,1024]{1,0:T(8,128)} %refs_1_.1, bf16[2,256,256]{2,1,0:T(8,128)(2,1)} %constant.10.clone.refs_2_, f32[2,8,1,128]{3,2,1,0:T(1,128)} %constant.11.clone.refs_3_, ...), custom_call_target="tpu_custom_call" | custom-call | tf_op jit(solution)/shard_map/substep/pallas_call | solution.py:453
  43.7 0.7 %store.1 = (f32[3,1,2,8,1024]{4,3,2,1,0:T(8,128)}, f32[1,2,8,1024]{3,2,1,0:T(8,128)}) custom-call(f32[3,1,2,8,1024]{4,3,2,1,0:T(8,128)S(1)} %get-tuple-element.4.following, f32[1,2,8,1024]{3,2,1,0:T(8,128)S(1)} %get-tuple-element.5.divergence), custom_call_target="tpu_custom_call" | custom-call | tf_op jit(solution)/shard_map/store/pallas_call | solution.py:475
